TPU v7x, 128 devices: a whole 4x4x4 slice. The times are simulated.
128 devices in a mesh: tp: 2 (over core), fsdp: 64 (over z, y, x).
Axes of the slice: x: 4, y: 4, z: 4, core: 2. Of those that a mesh axis runs over, the one named last changes fastest.
Arguments:
- x: bfloat16 [128, 1024, 1024], P('fsdp')
- grad_y: bfloat16 [128, 1024, 1024], P('fsdp')
- w_qkv: bfloat16 [1024, 3, 16, 64], P('fsdp', None, 'tp')
- w_out: bfloat16 [16, 64, 1024], P('tp', None, 'fsdp')
- w_ff: bfloat16 [1024, 2, 2816], P('fsdp', None, 'tp')
- w_down: bfloat16 [2816, 1024], P('tp', 'fsdp')
Outputs:
- output 1: bfloat16 [128, 1024, 1024], P('fsdp')
- output 2: bfloat16 [128, 1024, 1024], P('fsdp')
- output 3: float32 [1024, 3, 16, 64], P('fsdp', None, 'tp')
- output 4: float32 [16, 64, 1024], P('tp', None, 'fsdp')
- output 5: float32 [1024, 2, 2816], P('fsdp', None, 'tp')
- output 6: float32 [2816, 1024], P('tp', 'fsdp')
All inputs are finite; a program needn't handle non-finite values.
Results may differ from a plain program's by a relative error of at most 0.0160394.
Values are sent between devices in bfloat16 or wider.
A program may use at most 1 GiB of HBM per device.

v0:
```python
import jax
import jax.numpy as jnp
from jax import lax
from jax.sharding import PartitionSpec as P


def layer_norm(values):
    mean_val = jnp.mean(values, axis=-1, keepdims=True)
    centered = values - mean_val
    inv_std = lax.rsqrt(jnp.mean(centered * centered, axis=-1, keepdims=True) + 1e-5)
    return centered * inv_std, inv_std


def norm_backward(grad_norm, normed, inv_std):
    grad_mean = jnp.mean(grad_norm, axis=-1, keepdims=True)
    proj_mean = jnp.mean(grad_norm * normed, axis=-1, keepdims=True)
    return inv_std * (grad_norm - grad_mean - normed * proj_mean)


def rope_tables(seq_len, head_dim):
    inv_freq = 10000.0 ** (-jnp.arange(0, head_dim, 2, dtype=jnp.float32) / head_dim)
    angles = jnp.arange(seq_len, dtype=jnp.float32)[:, None] * inv_freq[None, :]
    return jnp.cos(angles)[:, None, :], jnp.sin(angles)[:, None, :]


def rotate(values, cos_tab, sin_tab):
    half_dim = values.shape[-1] // 2
    x_first = values[..., :half_dim]
    x_second = values[..., half_dim:]
    return jnp.concatenate([x_first * cos_tab - x_second * sin_tab, x_second * cos_tab + x_first * sin_tab], axis=-1)


def gather_fsdp(weight, dim_index):
    return lax.all_gather(weight, 'fsdp', axis=dim_index, tiled=True)


def scatter_fsdp(grad_part, dim_index):
    return lax.psum_scatter(grad_part, 'fsdp', scatter_dimension=dim_index, tiled=True)


def device_step(x, grad_y, w_qkv, w_out, w_ff, w_down):
    seq_len = x.shape[1]
    head_dim = w_qkv.shape[3]
    score_scale = head_dim ** -0.5
    cos_tab, sin_tab = rope_tables(seq_len, head_dim)
    causal = jnp.arange(seq_len)[:, None] >= jnp.arange(seq_len)[None, :]

    x_f32 = x.astype(jnp.float32)
    normed1, inv_std1 = layer_norm(x_f32)
    normed1_b = normed1.astype(jnp.bfloat16)
    qkv_full = gather_fsdp(w_qkv, 0)
    qkv_raw = jnp.einsum('btd,dchn->btchn', normed1_b, qkv_full, preferred_element_type=jnp.float32)
    clip_keep = jnp.abs(qkv_raw) < 8.0
    qkv_cl = jnp.clip(qkv_raw, -8.0, 8.0)
    q_rot = rotate(qkv_cl[:, :, 0], cos_tab, sin_tab).astype(jnp.bfloat16)
    k_rot = rotate(qkv_cl[:, :, 1], cos_tab, sin_tab).astype(jnp.bfloat16)
    v_val = qkv_cl[:, :, 2].astype(jnp.bfloat16)
    scores = jnp.einsum('bqhe,bkhe->bhqk', q_rot, k_rot, preferred_element_type=jnp.float32) * score_scale
    prob_f32 = jax.nn.softmax(jnp.where(causal, scores, -1e30), axis=-1)
    prob_b16 = prob_f32.astype(jnp.bfloat16)
    attn_o = jnp.einsum('bhqk,bkhe->bqhe', prob_b16, v_val, preferred_element_type=jnp.float32).astype(jnp.bfloat16)
    out_full = gather_fsdp(w_out, 2)
    attn_part = jnp.einsum('crif,ife->cre', attn_o, out_full, preferred_element_type=jnp.float32)
    hidden = (x_f32 + lax.psum(attn_part, 'tp')).astype(jnp.bfloat16)
    hidden_f32 = hidden.astype(jnp.float32)
    normed2, inv_std2 = layer_norm(hidden_f32)
    normed2_b = normed2.astype(jnp.bfloat16)
    ff_full = gather_fsdp(w_ff, 0)
    up_gate = jnp.einsum('btd,dcf->btcf', normed2_b, ff_full, preferred_element_type=jnp.float32)
    up_val = up_gate[:, :, 0]
    gate_val = up_gate[:, :, 1]
    gate_sig = jax.nn.sigmoid(gate_val)
    gate_act = gate_val * gate_sig
    mlp_act = (gate_act * up_val).astype(jnp.bfloat16)
    down_full = gather_fsdp(w_down, 1)
    mlp_part = jnp.einsum('btf,fd->btd', mlp_act, down_full, preferred_element_type=jnp.float32)
    y_out = (hidden_f32 + lax.psum(mlp_part, 'tp')).astype(jnp.bfloat16)

    grad_y32 = grad_y.astype(jnp.float32)
    grad_down = scatter_fsdp(jnp.einsum('btf,btd->fd', mlp_act, grad_y, preferred_element_type=jnp.float32), 1)
    down_again = gather_fsdp(w_down, 1)
    grad_act = jnp.einsum('btd,fd->btf', grad_y, down_again, preferred_element_type=jnp.float32)
    grad_up = grad_act * gate_act
    grad_gate = grad_act * up_val * gate_sig * (1.0 + gate_val * (1.0 - gate_sig))
    grad_upgate = jnp.stack([grad_up, grad_gate], axis=2).astype(jnp.bfloat16)
    grad_ff = scatter_fsdp(jnp.einsum('btd,btcf->dcf', normed2_b, grad_upgate, preferred_element_type=jnp.float32), 0)
    ff_again = gather_fsdp(w_ff, 0)
    grad_norm2 = lax.psum(jnp.einsum('btcf,dcf->btd', grad_upgate, ff_again, preferred_element_type=jnp.float32), 'tp')
    grad_hidden = grad_y32 + norm_backward(grad_norm2, normed2, inv_std2)
    grad_hidden_b = grad_hidden.astype(jnp.bfloat16)
    grad_out = scatter_fsdp(jnp.einsum('crif,cre->ife', attn_o, grad_hidden_b, preferred_element_type=jnp.float32), 2)
    out_again = gather_fsdp(w_out, 2)
    grad_o = jnp.einsum('cre,ife->crif', grad_hidden_b, out_again, preferred_element_type=jnp.float32).astype(jnp.bfloat16)
    grad_prob = jnp.einsum('bqhe,bkhe->bhqk', grad_o, v_val, preferred_element_type=jnp.float32)
    grad_v = jnp.einsum('bhqk,bqhe->bkhe', prob_b16, grad_o, preferred_element_type=jnp.float32)
    grad_score = prob_f32 * (grad_prob - jnp.sum(grad_prob * prob_f32, axis=-1, keepdims=True))
    grad_score_b = (grad_score * score_scale).astype(jnp.bfloat16)
    grad_q = jnp.einsum('bhqk,bkhe->bqhe', grad_score_b, k_rot, preferred_element_type=jnp.float32)
    grad_k = jnp.einsum('bhqk,bqhe->bkhe', grad_score_b, q_rot, preferred_element_type=jnp.float32)
    grad_qkv_all = jnp.stack([rotate(grad_q, cos_tab, -sin_tab), rotate(grad_k, cos_tab, -sin_tab), grad_v], axis=2)
    grad_qkv_b = jnp.where(clip_keep, grad_qkv_all, 0.0).astype(jnp.bfloat16)
    grad_qkv = scatter_fsdp(jnp.einsum('btd,btchn->dchn', normed1_b, grad_qkv_b, preferred_element_type=jnp.float32), 0)
    qkv_again = gather_fsdp(w_qkv, 0)
    grad_norm1 = lax.psum(jnp.einsum('btchn,dchn->btd', grad_qkv_b, qkv_again, preferred_element_type=jnp.float32), 'tp')
    grad_x = (grad_hidden + norm_backward(grad_norm1, normed1, inv_std1)).astype(jnp.bfloat16)
    return y_out, grad_x, grad_qkv, grad_out, grad_ff, grad_down


def solution(mesh):
    act_spec = P('fsdp', None, None)
    weight_specs = (P('fsdp', None, 'tp', None), P('tp', None, 'fsdp'), P('fsdp', None, 'tp'), P('tp', 'fsdp'))
    return jax.shard_map(device_step, mesh=mesh, in_specs=(act_spec, act_spec) + weight_specs, out_specs=(act_spec, act_spec) + weight_specs, check_vma=False)
```

profile of v0, /device:TPU:0, one launch (start us, length us, event | category | flops | bytes accessed | tf_op | source)
XLA Modules:
  0.0 2128.2 jit_solution(17467526115283898696)
XLA Ops:
  7.2 1.5 copy.12
  10.9 3.1 convert_reduce_fusion.1
  14.1 1.4 fusion.41
  16.7 81.3 %all-gather.5.cloned.1.call-done = bf16[1024,3,8,64]{3,0,2,1:T(8,128)(2,1)} async-done(((bf16[16,3,8,64]{3,0,2,1:T(8,128)(2,1)}), bf16[1024,3,8,64]{3,0,2,1:T(8,128)(2,1)}) %all-gather.5.cloned.1.call-update) | async-done | bytes 3145744 | tf_op jit(solution)/shard_map/all_gather | solution.py:34
  98.0 16.1 fusion.73
  114.1 12.1 copy_clamp_fusion
  126.2 4.3 slice_bitcast_fusion.3
  130.5 2.5 subtract_convert_fusion.1
  133.0 32.6 %fusion.133 = (f32[2,8,1024]{2,1,0:T(8,128)S(1)}, f32[2,8,1024,1024]{2,3,1,0:T(8,128)}) fusion(pred[1024,1024]{0,1:T(8,128)(4,1)} %iota_compare_fusion, bf16[2,1024,8,32]{1,3,2,0:T(8,128)(2,1)S(1)} %get-tuple-element.35, bf16[2,1024,8,32]{1,3,2,0:T(8,128)(2,1)} %get-tuple-element.36, bf16[2,1024,8,32]{1,3,2,0:T(8,128)(2,1)S(1)} %get-tuple-element.30, ...), kind=kOutput, calls=%fused_computation.149 | convolution fusion | flops 2222982144 | bytes 72417280 | tf_op jit(solution)/shard_map/sub | solution.py:59
  165.6 23.3 %fusion.99 = bf16[2,8,64,1024]{3,2,1,0:T(8,128)(2,1)S(1)} fusion(f32[2,1024,3,8,64]{1,4,3,0,2:T(8,128)} %copy_clamp_fusion, f32[2,8,1024,1024]{2,3,1,0:T(8,128)} %get-tuple-element.41, f32[2,8,1024]{2,1,0:T(8,128)S(1)} %get-tuple-element.40), kind=kOutput, calls=%fused_computation.118 | convolution fusion | flops 2182086656 | bytes 71368704 | tf_op jit(solution)/shard_map/bhqk,bkhe->bqhe/dot_general | solution.py:61
  190.2 8.4 convolution_bitcast_fusion.2
  200.8 40.7 %all-reduce.5.cloned.1.call-done = f32[2,1024,1024]{2,1,0:T(8,128)} async-done(((f32[2,1024,1024]{2,1,0:T(8,128)}), f32[2,1024,1024]{2,1,0:T(8,128)}) %all-reduce.5.cloned.1.call-update) | async-done | bytes 8388624 | tf_op jit(solution)/shard_map/psum | solution.py:64
  241.5 5.6 convert_reduce_fusion
  247.2 2.0 copy-done.3
  249.2 1.8 fusion.35
  251.0 66.2 %all-gather.9.cloned.1.call-done = bf16[1024,2,1408]{2,0,1:T(8,128)(2,1)} async-done(((bf16[16,2,1408]{2,0,1:T(8,128)(2,1)}), bf16[1024,2,1408]{2,0,1:T(8,128)(2,1)}) %all-gather.9.cloned.1.call-update) | async-done | bytes 5767184 | tf_op jit(solution)/shard_map/all_gather | solution.py:34
  317.2 20.2 fusion.55
  337.4 48.0 %all-gather.11.cloned.1.call-done = bf16[1408,1024]{0,1:T(8,128)(2,1)} async-done(((bf16[1408,16]{0,1:T(8,128)(2,1)}), bf16[1408,1024]{0,1:T(8,128)(2,1)}) %all-gather.11.cloned.1.call-update) | async-done | bytes 2883600 | tf_op jit(solution)/shard_map/all_gather | solution.py:34
  385.4 19.8 fusion.53
  405.2 18.1 fusion.68
  423.3 39.4 %all-reduce.7.cloned.1.call-done = f32[2,1024,1024]{2,1,0:T(8,128)} async-done(((f32[2,1024,1024]{2,1,0:T(8,128)}), f32[2,1024,1024]{2,1,0:T(8,128)}) %all-reduce.7.cloned.1.call-update) | async-done | bytes 8388624 | tf_op jit(solution)/shard_map/psum | solution.py:88
  462.7 6.1 fusion.131
  468.9 2.2 copy-done.7
  471.0 5.0 fusion.34
  476.1 3.2 copy-done.6
  479.3 2.5 fusion.102
  481.8 24.6 %fusion.83 = bf16[2,1024,1,8,64]{1,4,3,2,0:T(8,128)(2,1)} fusion(bf16[2,1024,8,64]{1,3,2,0:T(8,128)(2,1)S(1)} %fusion.102, f32[2,8,1024,1024]{2,3,1,0:T(8,128)} %get-tuple-element.41, f32[2,8,1024]{2,1,0:T(8,128)S(1)} %get-tuple-element.40), kind=kOutput, calls=%fused_computation.98 | convolution fusion | flops 2181038080 | bytes 71368704 | tf_op jit(solution)/shard_map/bhqk,bqhe->bkhe/dot_general | solution.py:95
  506.4 25.5 %fusion.107 = f32[2,8,1024,1024]{2,3,1,0:T(8,128)} fusion(bf16[2,1024,8,64]{1,3,2,0:T(8,128)(2,1)S(1)} %fusion.102, f32[2,1024,3,8,64]{1,4,3,0,2:T(8,128)} %copy_clamp_fusion), kind=kOutput, calls=%fused_computation.120 | convolution fusion | flops 2147483648 | bytes 71303168 | tf_op jit(solution)/shard_map/bqhe,bkhe->bhqk/dot_general | solution.py:94
  531.8 82.9 %fusion.86 = f32[2,1024,8,64]{1,3,2,0:T(8,128)} fusion(f32[2,8,1024,1024]{2,3,1,0:T(8,128)} %fusion.107, bf16[2,1024,8,32]{1,3,2,0:T(8,128)(2,1)S(1)} %copy-done.17, bf16[2,1024,8,32]{1,3,2,0:T(8,128)(2,1)} %get-tuple-element.36, f32[2,8,1024,1024]{2,3,1,0:T(8,128)} %get-tuple-element.41, f32[2,8,1024]{2,1,0:T(8,128)S(1)} %get-tuple-element.40), kind=kOutput, calls=%fused_computation.99 | convolution fusion | flops 2269135872 | bytes 140574720 | tf_op jit(solution)/shard_map/bhqk,bkhe->bqhe/dot_general | solution.py:98
  614.8 83.0 %fusion.89 = f32[2,1024,8,64]{1,3,2,0:T(8,128)} fusion(f32[2,8,1024,1024]{2,3,1,0:T(8,128)} %fusion.107, bf16[2,1024,8,32]{1,3,2,0:T(8,128)(2,1)S(1)} %copy-done.15, bf16[2,1024,8,32]{1,3,2,0:T(8,128)(2,1)S(1)} %copy-done.13, f32[2,8,1024,1024]{2,3,1,0:T(8,128)} %get-tuple-element.41, f32[2,8,1024]{2,1,0:T(8,128)S(1)} %get-tuple-element.40), kind=kOutput, calls=%fused_computation.100 | convolution fusion | flops 2269135872 | bytes 140574720 | tf_op jit(solution)/shard_map/bhqk,bqhe->bkhe/dot_general | solution.py:99
  697.8 4.8 multiply_subtract_fusion.1
  703.3 1.3 copy-done.8
  706.4 18.3 convolution_bitcast_fusion.1
  725.5 20.1 fusion.48
  745.7 12.7 fusion.76
  758.3 17.8 fusion.65
  776.2 12.2 convolution_bitcast_fusion
  788.5 8.3 fusion.80
  796.8 162.4 %reduce-scatter.5.cloned.1.call-done = f32[16,3,8,64]{3,0,2,1:T(8,128)} async-done(((f32[1024,3,8,64]{3,0,2,1:T(8,128)}), f32[16,3,8,64]{3,0,2,1:T(8,128)}) %reduce-scatter.5.cloned.1.call-update) | async-done | bytes 98320 | tf_op jit(solution)/shard_map/reduce_scatter | solution.py:38
  959.2 1.7 copy.29
  960.9 375.9 %reduce-scatter.9.cloned.1.call-done = f32[16,2,1408]{2,0,1:T(8,128)} async-done(((f32[1024,2,1408]{2,0,1:T(8,128)}), f32[16,2,1408]{2,0,1:T(8,128)}) %reduce-scatter.9.cloned.1.call-update) | async-done | bytes 180240 | tf_op jit(solution)/shard_map/reduce_scatter | solution.py:38
  1336.8 1.7 copy.30
  1338.5 55.9 %all-reduce.9.cloned.1.call-done = (f32[2,1024,1024]{2,1,0:T(8,128)}, f32[2,1024,1024]{2,1,0:T(8,128)}) async-done(((f32[2,1024,1024]{2,1,0:T(8,128)}, f32[2,1024,1024]{2,1,0:T(8,128)}), (f32[2,1024,1024]{2,1,0:T(8,128)}, f32[2,1024,1024]{2,1,0:T(8,128)})) %all-reduce.9.cloned.1.call-update) | async-done | bytes 16777232 | tf_op jit(solution)/shard_map/psum | solution.py:77
  1394.3 5.9 fusion.130
  1400.3 7.2 fusion.43
  1407.5 8.7 fusion.40
  1416.2 346.4 %reduce-scatter.11.cloned.1.call-done = f32[1408,16]{0,1:T(8,128)} async-done(((f32[1408,1024]{0,1:T(8,128)}), f32[1408,16]{0,1:T(8,128)}) %reduce-scatter.11.cloned.1.call-update) | async-done | bytes 90128 | tf_op jit(solution)/shard_map/reduce_scatter | solution.py:38
  1762.6 358.8 %reduce-scatter.7.cloned.1.call-done = f32[8,64,16]{1,2,0:T(8,128)} async-done(((f32[8,64,1024]{1,2,0:T(8,128)}), f32[8,64,16]{1,2,0:T(8,128)}) %reduce-scatter.7.cloned.1.call-update) | async-done | bytes 32784 | tf_op jit(solution)/shard_map/reduce_scatter | solution.py:38
  (100 shorter events, 10.3 us)
Async XLA Ops:
  7.2 90.9 %all-gather.5.cloned.1.call-start = ((), (), s32[]{:S(2)}) async-start(), calls=%async_computation.4 | async-start | bytes 6389760 | tf_op jit(solution)/shard_map/all_gather | solution.py:34
  8.8 180.2 %all-gather.7.cloned.1.call-start = ((), (), s32[]{:S(2)}) async-start(), calls=%async_computation.5 | async-start | bytes 2129920 | tf_op jit(solution)/shard_map/all_gather | solution.py:34
  9.5 232.0 %all-reduce.5.cloned.1.call-start = ((), (), s32[]{:S(2)}) async-start(), calls=%async_computation.6 | async-start | bytes 16777216 | tf_op jit(solution)/shard_map/psum | solution.py:64
  9.6 4.5 copy-start
  14.1 100.0 %copy-start.19 = (f32[2,1024]{1,0:T(2,128)}, f32[2,1024]{1,0:T(2,128)S(1)}, u32[]{:S(2)}) copy-start(f32[2,1024]{1,0:T(2,128)S(1)} %broadcast_multiply_fusion.5) | copy-start | bytes 24580
  15.5 98.6 %copy-start.24 = (f32[2,1024]{1,0:T(2,128)}, f32[2,1024]{1,0:T(2,128)S(1)}, u32[]{:S(2)}) copy-start(f32[2,1024]{1,0:T(2,128)S(1)} %add_rsqrt_fusion.1) | copy-start | bytes 24580
  16.7 113.8 %copy-start.10 = (f32[1024,32]{0,1:T(8,128)}, f32[1024,32]{0,1:T(8,128)S(1)}, u32[]{:S(2)}) copy-start(f32[1024,32]{0,1:T(8,128)S(1)} %get-tuple-element.39) | copy-start | bytes 393220
  133.0 32.7 %copy-start.12 = (bf16[2,1024,8,32]{1,3,2,0:T(8,128)(2,1)}, bf16[2,1024,8,32]{1,3,2,0:T(8,128)(2,1)S(1)}, u32[]{:S(2)}) copy-start(bf16[2,1024,8,32]{1,3,2,0:T(8,128)(2,1)S(1)} %get-tuple-element.29) | copy-start | bytes 3145732
  133.0 32.7 %copy-start.14 = (bf16[2,1024,8,32]{1,3,2,0:T(8,128)(2,1)}, bf16[2,1024,8,32]{1,3,2,0:T(8,128)(2,1)S(1)}, u32[]{:S(2)}) copy-start(bf16[2,1024,8,32]{1,3,2,0:T(8,128)(2,1)S(1)} %get-tuple-element.30) | copy-start | bytes 3145732
  133.0 32.7 %copy-start.16 = (bf16[2,1024,8,32]{1,3,2,0:T(8,128)(2,1)}, bf16[2,1024,8,32]{1,3,2,0:T(8,128)(2,1)S(1)}, u32[]{:S(2)}) copy-start(bf16[2,1024,8,32]{1,3,2,0:T(8,128)(2,1)S(1)} %get-tuple-element.35) | copy-start | bytes 3145732
  188.9 1.3 copy-start.29
  198.6 0.9 copy-start.23
  198.6 118.5 %all-gather.9.cloned.1.call-start = ((), (), s32[]{:S(2)}) async-start(), calls=%async_computation.7 | async-start | bytes 5857280 | tf_op jit(solution)/shard_map/all_gather | solution.py:34
  200.2 185.2 %all-gather.11.cloned.1.call-start = ((), (), s32[]{:S(2)}) async-start(), calls=%async_computation.8 | async-start | bytes 2928640 | tf_op jit(solution)/shard_map/all_gather | solution.py:34
  200.8 261.9 %all-reduce.7.cloned.1.call-start = ((), (), s32[]{:S(2)}) async-start(), calls=%async_computation.9 | async-start | bytes 16777216 | tf_op jit(solution)/shard_map/psum | solution.py:88
  247.1 2.0 copy-start.3
  247.2 221.7 %copy-start.21 = (f32[2,1024]{1,0:T(2,128)}, f32[2,1024]{1,0:T(2,128)S(1)}, u32[]{:S(2)}) copy-start(f32[2,1024]{1,0:T(2,128)S(1)} %broadcast_multiply_fusion.4) | copy-start | bytes 24580
  251.0 217.9 %copy-start.26 = (f32[2,1024]{1,0:T(2,128)}, f32[2,1024]{1,0:T(2,128)S(1)}, u32[]{:S(2)}) copy-start(f32[2,1024]{1,0:T(2,128)S(1)} %add_rsqrt_fusion) | copy-start | bytes 24580
  423.3 535.9 %reduce-scatter.5.cloned.1.call-start = ((), (), s32[]{:S(2)}) async-start(), calls=%async_computation.10 | async-start | bytes 12779520 | tf_op jit(solution)/shard_map/reduce_scatter | solution.py:38
  462.7 6.1 copy-start.4
  462.7 8.3 copy-start.7
  471.0 8.2 copy-start.28
  476.1 3.2 copy-start.6
  506.4 25.5 %copy-start.17 = (bf16[2,1024,8,32]{1,3,2,0:T(8,128)(2,1)S(1)}, bf16[2,1024,8,32]{1,3,2,0:T(8,128)(2,1)}, u32[]{:S(2)}) copy-start(bf16[2,1024,8,32]{1,3,2,0:T(8,128)(2,1)} %copy-done.16) | copy-start | bytes 3145732
  531.8 83.0 %copy-start.13 = (bf16[2,1024,8,32]{1,3,2,0:T(8,128)(2,1)S(1)}, bf16[2,1024,8,32]{1,3,2,0:T(8,128)(2,1)}, u32[]{:S(2)}) copy-start(bf16[2,1024,8,32]{1,3,2,0:T(8,128)(2,1)} %copy-done.12) | copy-start | bytes 3145732
  531.8 83.0 %copy-start.15 = (bf16[2,1024,8,32]{1,3,2,0:T(8,128)(2,1)S(1)}, bf16[2,1024,8,32]{1,3,2,0:T(8,128)(2,1)}, u32[]{:S(2)}) copy-start(bf16[2,1024,8,32]{1,3,2,0:T(8,128)(2,1)} %copy-done.14) | copy-start | bytes 3145732
  614.8 83.0 %copy-start.11 = (f32[1024,32]{0,1:T(8,128)S(1)}, f32[1024,32]{0,1:T(8,128)}, u32[]{:S(2)}) copy-start(f32[1024,32]{0,1:T(8,128)} %copy-done.10) | copy-start | bytes 393220
  614.8 83.0 %copy-start.18 = (f32[1024,32]{0,1:T(8,128)S(1)}, f32[1024,32]{0,1:T(8,128)}, u32[]{:S(2)}) copy-start(f32[1024,32]{0,1:T(8,128)} %get-tuple-element.37) | copy-start | bytes 393220
  702.6 2.9 copy-start.1
  702.7 2.9 copy-start.20
  702.7 2.9 copy-start.25
  702.7 3.0 copy-start.31
  702.7 3.7 copy-start.32
  703.3 1.3 copy-start.8
  724.8 0.7 copy-start.22
  724.8 0.7 copy-start.27
  724.8 612.0 %reduce-scatter.9.cloned.1.call-start = ((), (), s32[]{:S(2)}) async-start(), calls=%async_computation.12 | async-start | bytes 11714560 | tf_op jit(solution)/shard_map/reduce_scatter | solution.py:38
  745.6 648.8 %all-reduce.9.cloned.1.call-start = ((), (), s32[]{:S(2)}) async-start(), calls=%async_computation.14 | async-start | bytes 33554432 | tf_op jit(solution)/shard_map/psum | solution.py:77
  745.6 12.7 copy-start.9
  745.6 12.7 copy-start.33
  776.2 12.3 copy-start.30
  776.2 986.4 %reduce-scatter.11.cloned.1.call-start = ((), (), s32[]{:S(2)}) async-start(), calls=%async_computation.13 | async-start | bytes 5857280 | tf_op jit(solution)/shard_map/reduce_scatter | solution.py:38
  788.4 1333.0 %reduce-scatter.7.cloned.1.call-start = ((), (), s32[]{:S(2)}) async-start(), calls=%async_computation.11 | async-start | bytes 4259840 | tf_op jit(solution)/shard_map/reduce_scatter | solution.py:38
  1394.3 5.9 copy-start.5
  1400.3 7.2 copy-start.2
Sparse Core Ops, SparseCore 0:
  11.2 86.7 all-gather.4
  100.7 66.9 all-gather.6
  198.8 42.7 all-reduce.4
  244.9 72.2 all-gather.8
  319.9 65.4 all-gather.10
  423.4 39.2 all-reduce.6
  724.9 234.2 reduce-scatter.4
  961.6 375.1 reduce-scatter.8
  1339.5 54.8 all-reduce.8
  1397.1 365.4 reduce-scatter.10
  1765.6 355.8 reduce-scatter.6
where the time goes:
time: 2140 us; the launch traced here: 2130 us
  waiting for transfers between devices  1580 us (74%)
  matrix products  446 us (21%)
  other arithmetic  67.3 us (3%)
  local copies, waits for them, and re-layouts  23.2 us (1%)
    reduce_scatter x4, waiting for transfers between devices, scatter_fsdp(): lax.psum_scatter(grad_part, 'fsdp', scatter_dimension=dim_index, tiled=True)  1240 us
    all_gather x4, waiting for transfers between devices, gather_fsdp(): return lax.all_gather(weight, 'fsdp', axis=dim_index, tiled=True)  196 us
    dot_general x1, matrix products, device_step(): jnp.einsum('bhqk,bqhe->bkhe', grad_score_b, q_rot, preferred_element_type...  83 us
    dot_general x1, matrix products, device_step(): jnp.einsum('bhqk,bkhe->bqhe', grad_score_b, k_rot, preferred_element_type...  82.9 us
    psum x1, waiting for transfers between devices, device_step(): y_out = (hidden_f32 + lax.psum(mlp_part, 'tp')).astype(jnp.bfloat16)  55.9 us
  transfers between devices with their start and end apart: 11, of which 10 were waited for; matrix products, arithmetic and copies ran while one was open for 10% of the time, Pallas kernels for 0%

commit v1 on v0

v1 whole, which is shorter than its diff:
```python
import functools
import jax, jax.numpy as jnp
from jax import lax
from jax.experimental import pallas as pl
from jax.experimental.pallas import tpu as pltpu
from jax.sharding import PartitionSpec as P

MESH_ID = pl.DeviceIdType.MESH
ORDERS = ((2, 1, 0), (1, 0, 2), (0, 2, 1))


class Torus:
    def __init__(self, send_sem, recv_sem):
        self.tp = lax.axis_index('tp')
        me = lax.axis_index('fsdp')
        self.at = (me // 16, (me // 4) % 4, me % 4)
        self.send_sem, self.recv_sem = send_sem, recv_sem
        self.n = 0
        self.sent = []

    def shift(self, axis, by):
        return (self.at[axis] + by + 4) % 4

    def peer(self, axis, by):
        pos = list(self.at)
        pos[axis] = self.shift(axis, by)
        return (self.tp, pos[0] * 16 + pos[1] * 4 + pos[2])

    def copy(self, src, dst, device):
        desc = pltpu.make_async_remote_copy(src, dst, self.send_sem.at[self.n], self.recv_sem.at[self.n], device_id=device, device_id_type=MESH_ID)
        self.n += 1
        self.sent.append(desc)
        return desc

    def local(self, src, dst):
        desc = pltpu.make_async_copy(src, dst, self.send_sem.at[self.n])
        self.n += 1
        return desc

    def barrier(self, partner=False):
        sem = pltpu.get_barrier_semaphore()
        peers = [self.peer(axis, by) for axis in range(3) for by in (1, -1)]
        if partner:
            peers.append((1 - self.tp, self.at[0] * 16 + self.at[1] * 4 + self.at[2]))
        for device in peers:
            pl.semaphore_signal(sem, inc=1, device_id=device, device_id_type=MESH_ID)
        pl.semaphore_wait(sem, len(peers))

    def finish(self):
        for desc in self.sent:
            desc.wait_send()
        self.sent = []


def window(ref, picks, rows, cols):
    return ref.at[picks[0], picks[1], picks[2], rows, cols]


def gather_stages(net, shards, outs, segs):
    whole = slice(None)
    state = {}

    def picks(order, phase, coord):
        got = [None] * 3
        for pos, axis in enumerate(order):
            got[axis] = pl.ds(0, 4) if pos < phase else net.at[axis]
        got[order[phase]] = coord
        return got

    def halves(order, phase, coord, off, width):
        if phase == 0:
            left = (width // 256) * 128 if width >= 256 else width
            parts = [(picks(order, phase, coord), pl.ds(off, left))]
            parts.append((picks(order, phase, coord), pl.ds(off + left, width - left)) if width > left else None)
            return parts
        parts = []
        for lo in (0, 2):
            got = picks(order, phase, coord)
            got[order[0]] = pl.ds(lo, 2)
            parts.append((got, pl.ds(off, width)))
        return parts

    def local_copies():
        state['own'] = []
        for shard, out in zip(shards, outs):
            desc = net.local(shard, out.at[net.at[0], net.at[1], net.at[2]])
            desc.start()
            state['own'].append(desc)

    def wait_own():
        for desc in state['own']:
            desc.wait()

    def start(phase):
        for colour, order in enumerate(ORDERS):
            axis = order[phase]
            for seg, (arr, off, width) in enumerate(segs[colour]):
                where = picks(order, phase, net.at[axis])
                dst = window(outs[arr], where, whole, pl.ds(off, width))
                src = shards[arr].at[:, pl.ds(off, width)] if phase == 0 else dst
                for by in (1, -1):
                    desc = net.copy(src, dst, net.peer(axis, by))
                    desc.start()
                    state[colour, phase, seg, by] = desc

    def forward(phase):
        for by in (1, -1):
            for colour, order in enumerate(ORDERS):
                axis = order[phase]
                for seg, (arr, off, width) in enumerate(segs[colour]):
                    state[colour, phase, seg, by].wait_recv()
                    part = halves(order, phase, net.shift(axis, -by), off, width)[0 if by == 1 else 1]
                    if part is None:
                        continue
                    ref = window(outs[arr], part[0], whole, part[1])
                    desc = net.copy(ref, ref, net.peer(axis, by))
                    desc.start()
                    state[colour, phase, seg, 'f', by] = desc

    def settle(phase):
        for by in (1, -1):
            for colour in range(3):
                for seg in range(len(segs[colour])):
                    if (colour, phase, seg, 'f', by) in state:
                        state[colour, phase, seg, 'f', by].wait_recv()

    def first():
        local_copies()
        start(0)

    def second():
        settle(0)
        wait_own()
        start(1)

    def third():
        settle(1)
        start(2)

    def last():
        settle(2)
        net.finish()

    return [first, functools.partial(forward, 0), second, functools.partial(forward, 1), third, functools.partial(forward, 2), last]


def gather_kernel(n_arr, segs, *refs):
    shards, outs = refs[:n_arr], refs[n_arr:2 * n_arr]
    send_sem, recv_sem = refs[2 * n_arr:]
    net = Torus(send_sem, recv_sem)
    net.barrier()
    for stage in gather_stages(net, shards, outs, segs):
        stage()


def all_gather(shards, segs, collective_id, sems=160):
    n_arr = len(shards)
    outs = [jax.ShapeDtypeStruct((4, 4, 4) + s.shape, s.dtype) for s in shards]
    got = pl.pallas_call(
        functools.partial(gather_kernel, n_arr, segs),
        out_shape=outs,
        in_specs=[pl.BlockSpec(memory_space=pltpu.VMEM)] * n_arr,
        out_specs=[pl.BlockSpec(memory_space=pltpu.HBM)] * n_arr,
        scratch_shapes=[pltpu.SemaphoreType.DMA((sems,)), pltpu.SemaphoreType.DMA((sems,))],
        compiler_params=pltpu.CompilerParams(collective_id=collective_id, has_side_effects=True),
        name='torus_gather',
    )(*shards)
    return [g.reshape(-1, g.shape[-1]) for g in got]


def scatter_buffers(widths):
    shapes = []
    for w in widths:
        shapes += [
            (2, 2, 4, 16, w), (2, 2, 4, 16, w), (2, 2, 4, 16, w), (2, 2, 4, 16, w), (4, 4, 16, w),
            (3, 2, 2, 16, w), (3, 2, 8, w),
        ]
    return [pltpu.VMEM(s, jnp.float32) for s in shapes]


def scatter_stages(net, parts, outs, segs, bufs):
    state = {}
    rows = slice(None)

    def buf(colour):
        return bufs[7 * colour:7 * colour + 7]

    def rest(order):
        return sorted(order[1:])

    def src1(order, coord, half):
        got = [pl.ds(0, 4)] * 3
        got[order[0]] = coord
        if half is not None:
            got[rest(order)[0]] = pl.ds(2 * half, 2)
        return got

    def part1(colour, seg, coord, half):
        arr, off, width = segs[colour][seg]
        return window(parts[arr], src1(ORDERS[colour], coord, half), rows, pl.ds(off, width))

    def spans(colour):
        at = 0
        for seg, (_, _, width) in enumerate(segs[colour]):
            yield seg, pl.ds(at, width)
            at += width

    def start1():
        for kind in ('x', 'y'):
            for colour, order in enumerate(ORDERS):
                axis = order[0]
                xb, yb = buf(colour)[0], buf(colour)[1]
                for seg, cols in spans(colour):
                    for d, by in ((0, 1), (1, -1)):
                        if kind == 'x':
                            src, dst = part1(colour, seg, net.shift(axis, 2), d), xb.at[d, :, :, :, cols]
                        else:
                            src, dst = part1(colour, seg, net.shift(axis, by), 1 - d), yb.at[d, :, :, :, cols]
                        desc = net.copy(src, dst, net.peer(axis, by))
                        desc.start()
                        state[1, kind, colour, seg, d] = desc
        for colour, order in enumerate(ORDERS):
            axis = order[0]
            fb, rb = buf(colour)[3], buf(colour)[4]
            for seg, cols in spans(colour):
                for d, by in ((0, 1), (1, -1)):
                    desc = net.local(part1(colour, seg, net.shift(axis, by), d), fb.at[d, :, :, :, cols])
                    desc.start()
                    state[1, 'f', colour, seg, d] = desc
                desc = net.local(part1(colour, seg, net.at[axis], None), rb.at[:, :, :, cols])
                desc.start()
                state[1, 'r', colour, seg] = desc

    def relay1():
        for colour, order in enumerate(ORDERS):
            axis = order[0]
            xb, zb, fb = buf(colour)[0], buf(colour)[2], buf(colour)[3]
            for d, by in ((0, 1), (1, -1)):
                for seg, _ in spans(colour):
                    state[1, 'x', colour, seg, d].wait_recv()
                    state[1, 'f', colour, seg, d].wait()

                def body(i, carry, xb=xb, fb=fb, d=d):
                    fb[d, i // 4, i % 4] = fb[d, i // 4, i % 4] + xb[d, i // 4, i % 4]
                    return carry

                lax.fori_loop(0, 8, body, 0)
                desc = net.copy(fb.at[d], zb.at[d], net.peer(axis, by))
                desc.start()
                state[1, 'z', colour, d] = desc

    def merge1():
        for colour in range(3):
            yb, zb, rb = buf(colour)[1], buf(colour)[2], buf(colour)[4]
            for seg, _ in spans(colour):
                state[1, 'r', colour, seg].wait()
                for d in (0, 1):
                    state[1, 'y', colour, seg, d].wait_recv()
            for d in (0, 1):
                state[1, 'z', colour, d].wait_recv()

            def body(i, carry, yb=yb, zb=zb, rb=rb):
                b, c = i // 4, i % 4
                rb[b, c] = rb[b, c] + yb[1, b, c] + zb[0, b, c]
                rb[b + 2, c] = rb[b + 2, c] + yb[0, b, c] + zb[1, b, c]
                return carry

            lax.fori_loop(0, 8, body, 0)

    def block2(colour, coord, half):
        order = ORDERS[colour]
        rb = buf(colour)[4]
        keep = pl.ds(0, 4) if half is None else pl.ds(2 * half, 2)
        return rb.at[coord, keep] if rest(order)[0] == order[1] else rb.at[keep, coord]

    def piece2(colour, coord, i):
        order = ORDERS[colour]
        rb = buf(colour)[4]
        return rb.at[coord, i] if rest(order)[0] == order[1] else rb.at[i, coord]

    def start2():
        for kind in ('x', 'y'):
            for colour, order in enumerate(ORDERS):
                axis, b2 = order[1], buf(colour)[5]
                for d, by in ((0, 1), (1, -1)):
                    src = block2(colour, net.shift(axis, 2), d) if kind == 'x' else block2(colour, net.shift(axis, by), 1 - d)
                    desc = net.copy(src, b2.at[0 if kind == 'x' else 1, d], net.peer(axis, by))
                    desc.start()
                    state[2, kind, colour, d] = desc

    def relay2():
        for colour, order in enumerate(ORDERS):
            axis, b2 = order[1], buf(colour)[5]
            for d, by in ((0, 1), (1, -1)):
                state[2, 'x', colour, d].wait_recv()
                for i in range(2):
                    b2[0, d, i] = b2[0, d, i] + piece2(colour, net.shift(axis, by), 2 * d + i)[...]
                desc = net.copy(b2.at[0, d], b2.at[2, d], net.peer(axis, by))
                desc.start()
                state[2, 'z', colour, d] = desc

    def merge2():
        for colour, order in enumerate(ORDERS):
            axis, b2 = order[1], buf(colour)[5]
            for d in (0, 1):
                state[2, 'y', colour, d].wait_recv()
                state[2, 'z', colour, d].wait_recv()
            for i in range(2):
                lo, hi = piece2(colour, net.at[axis], i), piece2(colour, net.at[axis], 2 + i)
                lo[...] = lo[...] + b2[1, 1, i] + b2[2, 0, i]
                hi[...] = hi[...] + b2[1, 0, i] + b2[2, 1, i]

    def block3(colour, coord, half):
        order = ORDERS[colour]
        ref = piece2(colour, net.at[order[1]], coord)
        return ref if half is None else ref.at[pl.ds(8 * half, 8)]

    def start3():
        for kind in ('x', 'y'):
            for colour, order in enumerate(ORDERS):
                axis, b3 = order[2], buf(colour)[6]
                for d, by in ((0, 1), (1, -1)):
                    src = block3(colour, net.shift(axis, 2), d) if kind == 'x' else block3(colour, net.shift(axis, by), 1 - d)
                    desc = net.copy(src, b3.at[0 if kind == 'x' else 1, d], net.peer(axis, by))
                    desc.start()
                    state[3, kind, colour, d] = desc

    def relay3():
        for colour, order in enumerate(ORDERS):
            axis, b3 = order[2], buf(colour)[6]
            for d, by in ((0, 1), (1, -1)):
                state[3, 'x', colour, d].wait_recv()
                b3[0, d] = b3[0, d] + block3(colour, net.shift(axis, by), d)[...]
                desc = net.copy(b3.at[0, d], b3.at[2, d], net.peer(axis, by))
                desc.start()
                state[3, 'z', colour, d] = desc

    def merge3():
        for colour, order in enumerate(ORDERS):
            axis, b3 = order[2], buf(colour)[6]
            for d in (0, 1):
                state[3, 'y', colour, d].wait_recv()
                state[3, 'z', colour, d].wait_recv()
            lo, hi = block3(colour, net.at[axis], 0), block3(colour, net.at[axis], 1)
            low = lo[...] + b3[1, 1] + b3[2, 0]
            high = hi[...] + b3[1, 0] + b3[2, 1]
            at = 0
            for arr, off, width in segs[colour]:
                outs[arr][pl.ds(0, 8), pl.ds(off, width)] = low[:, at:at + width]
                outs[arr][pl.ds(8, 8), pl.ds(off, width)] = high[:, at:at + width]
                at += width
        net.finish()

    def join(*fns):
        def run():
            for fn in fns:
                fn()
        return run

    return [start1, relay1, join(merge1, start2), relay2, join(merge2, start3), relay3, merge3]


def scatter_kernel(n_arr, segs, *refs):
    parts, outs = refs[:n_arr], refs[n_arr:2 * n_arr]
    send_sem, recv_sem = refs[2 * n_arr:2 * n_arr + 2]
    bufs = refs[2 * n_arr + 2:]
    net = Torus(send_sem, recv_sem)
    net.barrier()
    for stage in scatter_stages(net, parts, outs, segs, bufs):
        stage()


def reduce_scatter(parts, segs, collective_id, sems=160):
    n_arr = len(parts)
    widths = [sum(w for _, _, w in seg) for seg in segs]
    return pl.pallas_call(
        functools.partial(scatter_kernel, n_arr, segs),
        out_shape=[jax.ShapeDtypeStruct((16, p.shape[-1]), jnp.float32) for p in parts],
        in_specs=[pl.BlockSpec(memory_space=pltpu.HBM)] * n_arr,
        out_specs=[pl.BlockSpec(memory_space=pltpu.VMEM)] * n_arr,
        scratch_shapes=[pltpu.SemaphoreType.DMA((sems,)), pltpu.SemaphoreType.DMA((sems,))] + scatter_buffers(widths),
        compiler_params=pltpu.CompilerParams(collective_id=collective_id, has_side_effects=True, vmem_limit_bytes=60 * 2**20),
        name='torus_scatter',
    )(*[p.reshape(4, 4, 4, 16, p.shape[-1]) for p in parts])


SEGS = (((2, 0, 2048),), ((2, 2048, 768), (3, 0, 1280)), ((3, 1280, 128), (1, 0, 512), (0, 0, 1536)))


def layer_norm(values):
    mean_val = jnp.mean(values, axis=-1, keepdims=True)
    centered = values - mean_val
    inv_std = lax.rsqrt(jnp.mean(centered * centered, axis=-1, keepdims=True) + 1e-5)
    return centered * inv_std, inv_std


def norm_backward(grad_norm, normed, inv_std):
    grad_mean = jnp.mean(grad_norm, axis=-1, keepdims=True)
    proj_mean = jnp.mean(grad_norm * normed, axis=-1, keepdims=True)
    return inv_std * (grad_norm - grad_mean - normed * proj_mean)


def rope_tables(seq_len, head_dim):
    inv_freq = 10000.0 ** (-jnp.arange(0, head_dim, 2, dtype=jnp.float32) / head_dim)
    angles = jnp.arange(seq_len, dtype=jnp.float32)[:, None] * inv_freq[None, :]
    return jnp.cos(angles)[:, None, :], jnp.sin(angles)[:, None, :]


def rotate(values, cos_tab, sin_tab):
    half_dim = values.shape[-1] // 2
    x_first = values[..., :half_dim]
    x_second = values[..., half_dim:]
    return jnp.concatenate([x_first * cos_tab - x_second * sin_tab, x_second * cos_tab + x_first * sin_tab], axis=-1)


def device_step(x, grad_y, w_qkv, w_out, w_ff, w_down):
    seq_len = x.shape[1]
    head_dim = w_qkv.shape[3]
    score_scale = head_dim ** -0.5
    cos_tab, sin_tab = rope_tables(seq_len, head_dim)
    causal = jnp.arange(seq_len)[:, None] >= jnp.arange(seq_len)[None, :]

    heads = w_qkv.shape[2]
    ff = w_ff.shape[2]
    shards = [w_qkv.reshape(16, -1), w_out.reshape(heads * head_dim, 16).T, w_ff.reshape(16, -1), w_down.T]
    qkv_full, out_full, ff_full, down_full = all_gather(shards, SEGS, 0)
    qkv_full = qkv_full.reshape(-1, 3, heads, head_dim)
    out_full = out_full.reshape(-1, heads, head_dim)
    ff_full = ff_full.reshape(-1, 2, ff)

    x_f32 = x.astype(jnp.float32)
    normed1, inv_std1 = layer_norm(x_f32)
    normed1_b = normed1.astype(jnp.bfloat16)
    qkv_raw = jnp.einsum('btd,dchn->btchn', normed1_b, qkv_full, preferred_element_type=jnp.float32)
    clip_keep = jnp.abs(qkv_raw) < 8.0
    qkv_cl = jnp.clip(qkv_raw, -8.0, 8.0)
    q_rot = rotate(qkv_cl[:, :, 0], cos_tab, sin_tab).astype(jnp.bfloat16)
    k_rot = rotate(qkv_cl[:, :, 1], cos_tab, sin_tab).astype(jnp.bfloat16)
    v_val = qkv_cl[:, :, 2].astype(jnp.bfloat16)
    scores = jnp.einsum('bqhe,bkhe->bhqk', q_rot, k_rot, preferred_element_type=jnp.float32) * score_scale
    prob_f32 = jax.nn.softmax(jnp.where(causal, scores, -1e30), axis=-1)
    prob_b16 = prob_f32.astype(jnp.bfloat16)
    attn_o = jnp.einsum('bhqk,bkhe->bqhe', prob_b16, v_val, preferred_element_type=jnp.float32).astype(jnp.bfloat16)
    attn_part = jnp.einsum('crif,eif->cre', attn_o, out_full, preferred_element_type=jnp.float32)
    hidden = (x_f32 + lax.psum(attn_part, 'tp')).astype(jnp.bfloat16)
    hidden_f32 = hidden.astype(jnp.float32)
    normed2, inv_std2 = layer_norm(hidden_f32)
    normed2_b = normed2.astype(jnp.bfloat16)
    up_gate = jnp.einsum('btd,dcf->btcf', normed2_b, ff_full, preferred_element_type=jnp.float32)
    up_val = up_gate[:, :, 0]
    gate_val = up_gate[:, :, 1]
    gate_sig = jax.nn.sigmoid(gate_val)
    gate_act = gate_val * gate_sig
    mlp_act = (gate_act * up_val).astype(jnp.bfloat16)
    mlp_part = jnp.einsum('btf,df->btd', mlp_act, down_full, preferred_element_type=jnp.float32)
    y_out = (hidden_f32 + lax.psum(mlp_part, 'tp')).astype(jnp.bfloat16)

    grad_y32 = grad_y.astype(jnp.float32)
    grad_down = jnp.einsum('btd,btf->df', grad_y, mlp_act, preferred_element_type=jnp.float32)
    grad_act = jnp.einsum('btd,df->btf', grad_y, down_full, preferred_element_type=jnp.float32)
    grad_up = grad_act * gate_act
    grad_gate = grad_act * up_val * gate_sig * (1.0 + gate_val * (1.0 - gate_sig))
    grad_upgate = jnp.stack([grad_up, grad_gate], axis=2).astype(jnp.bfloat16)
    grad_ff = jnp.einsum('btd,btcf->dcf', normed2_b, grad_upgate, preferred_element_type=jnp.float32)
    grad_norm2 = lax.psum(jnp.einsum('btcf,dcf->btd', grad_upgate, ff_full, preferred_element_type=jnp.float32), 'tp')
    grad_hidden = grad_y32 + norm_backward(grad_norm2, normed2, inv_std2)
    grad_hidden_b = grad_hidden.astype(jnp.bfloat16)
    grad_out = jnp.einsum('cre,crif->eif', grad_hidden_b, attn_o, preferred_element_type=jnp.float32)
    grad_o = jnp.einsum('cre,eif->crif', grad_hidden_b, out_full, preferred_element_type=jnp.float32).astype(jnp.bfloat16)
    grad_prob = jnp.einsum('bqhe,bkhe->bhqk', grad_o, v_val, preferred_element_type=jnp.float32)
    grad_v = jnp.einsum('bhqk,bqhe->bkhe', prob_b16, grad_o, preferred_element_type=jnp.float32)
    grad_score = prob_f32 * (grad_prob - jnp.sum(grad_prob * prob_f32, axis=-1, keepdims=True))
    grad_score_b = (grad_score * score_scale).astype(jnp.bfloat16)
    grad_q = jnp.einsum('bhqk,bkhe->bqhe', grad_score_b, k_rot, preferred_element_type=jnp.float32)
    grad_k = jnp.einsum('bhqk,bqhe->bkhe', grad_score_b, q_rot, preferred_element_type=jnp.float32)
    grad_qkv_all = jnp.stack([rotate(grad_q, cos_tab, -sin_tab), rotate(grad_k, cos_tab, -sin_tab), grad_v], axis=2)
    grad_qkv_b = jnp.where(clip_keep, grad_qkv_all, 0.0).astype(jnp.bfloat16)
    grad_qkv = jnp.einsum('btd,btchn->dchn', normed1_b, grad_qkv_b, preferred_element_type=jnp.float32)
    grad_norm1 = lax.psum(jnp.einsum('btchn,dchn->btd', grad_qkv_b, qkv_full, preferred_element_type=jnp.float32), 'tp')
    grad_x = (grad_hidden + norm_backward(grad_norm1, normed1, inv_std1)).astype(jnp.bfloat16)
    full = [g.reshape(1024, -1) for g in (grad_qkv, grad_out, grad_ff, grad_down)]
    own_qkv, own_out, own_ff, own_down = reduce_scatter(full, SEGS, 1)
    own_out = own_out.T.reshape(heads, head_dim, 16)
    return y_out, grad_x, own_qkv.reshape(16, 3, heads, head_dim), own_out, own_ff.reshape(16, 2, ff), own_down.T


def solution(mesh):
    act_spec = P('fsdp', None, None)
    weight_specs = (P('fsdp', None, 'tp', None), P('tp', None, 'fsdp'), P('fsdp', None, 'tp'), P('tp', 'fsdp'))
    return jax.shard_map(device_step, mesh=mesh, in_specs=(act_spec, act_spec) + weight_specs, out_specs=(act_spec, act_spec) + weight_specs, check_vma=False)
```

time: 2140 us -> 861 us (0.40)
  the two profiles are of different devices: /device:TPU:0 before, /device:TPU:1 now
where the time goes in v1:
time: 861 us; the launch traced here: 849 us
  matrix products  431 us (50%)
  Pallas kernels  170 us (20%)
  local copies, waits for them, and re-layouts  108 us (13%)
  other arithmetic  63.2 us (7%)
  waiting for transfers between devices  62 us (7%)
  between operations  14.8 us (2%)
    pallas_call x1, Pallas kernels, reduce_scatter(): pl.pallas_call(functools.partial(scatter_kernel, n_arr, segs), out_shape=...  108 us
    dot_general x1, matrix products, device_step(): jnp.einsum('bhqk,bkhe->bqhe', grad_score_b, k_rot, preferred_element_type...  83.4 us
    dot_general x1, matrix products, device_step(): jnp.einsum('bhqk,bqhe->bkhe', grad_score_b, q_rot, preferred_element_type...  82.9 us
    pallas_call x1, Pallas kernels, all_gather(): pl.pallas_call(functools.partial(gather_kernel, n_arr, segs), out_shape=o...  61.3 us
    psum x1, waiting for transfers between devices, device_step(): hidden = (x_f32 + lax.psum(attn_part, 'tp')).astype(jnp.bfloat16)  32.7 us
    sub x1, matrix products, device_step(): prob_f32 = jax.nn.softmax(jnp.where(causal, scores, -1e+30), axis=-1)  32.5 us
    another operation x3, local copies, waits for them, and re-layouts, reduce_scatter(): p.reshape(4, 4, 4, 16, p.shape[-1])  31.4 us
    psum x1, waiting for transfers between devices, device_step(): lax.psum(jnp.einsum('btcf,dcf->btd', grad_upgate, ff_full, preferred_elem...  29.3 us
  transfers between devices with their start and end apart: 3, of which 2 were waited for; matrix products, arithmetic and copies ran while one was open for 16% of the time, Pallas kernels for 13%

profile of v1, /device:TPU:1, one launch (start us, length us, event | category | flops | bytes accessed | tf_op | source)
XLA Modules:
  0.0 849.2 jit_solution(8642300694553204665)
XLA Ops:
  8.5 2.8 convert_reduce_fusion.1
  11.4 3.0 fusion.54
  17.7 61.3 %torus_gather.1 = (bf16[4,4,4,16,1536]{4,3,2,1,0:T(8,128)(2,1)}, bf16[4,4,4,16,512]{4,3,2,1,0:T(8,128)(2,1)}, bf16[4,4,4,16,2816]{4,3,2,1,0:T(8,128)(2,1)}, bf16[4,4,4,16,1408]{4,3,2,1,0:T(8,128)(2,1)}) custom-call(bf16[16,1536]{1,0:T(8,128)(2,1)} %reshape.149.refs_0_, bf16[16,512]{1,0:T(8,128)(2,1)} %bitcast.233, bf16[16,2816]{1,0:T(8,128)(2,1)} %bitcast.230, ...), custom_call_target="tpu_custom_call" | custom-call | tf_op jit(solution)/shard_map/torus_gather/pallas_call | solution.py:159
  79.0 2.8 reshape_reshape.19
  81.8 2.2 copy.43
  84.1 8.9 %reshape_reshape.18 = bf16[1024,3,8,64]{3,2,1,0:T(8,128)(2,1)} reshape(bf16[4,4,4,16,1536]{4,3,2,1,0:T(8,128)(2,1)} %get-tuple-element.14) | data formatting | bytes 6291456 | tf_op jit(solution)/shard_map/reshape;reshape | solution.py:427
  92.9 6.4 copy.40
  99.4 13.7 %fusion.93 = (u8[2,1024,3,64]{1,3,2,0:T(8,128)(4,1)}, f32[2,1024,3,8,64]{1,4,3,2,0:T(8,128)}) fusion(bf16[1024,3,8,64]{0,3,2,1:T(8,128)(2,1)S(1)} %copy.40, bf16[2,1024,1024]{2,1,0:T(8,128)(2,1)} %param.6, f32[2,1024]{1,0:T(2,128)S(1)} %add_rsqrt_fusion.1, f32[2,1024]{1,0:T(2,128)S(1)} %broadcast_multiply_fusion.5), kind=kOutput, calls=%fused_computation.110 | convolution fusion | flops 6469320704 | bytes 20332544 | tf_op jit(solution)/shard_map/btd,dchn->btchn/dot_general | solution.py:434
  113.1 12.1 %copy_clamp_fusion = f32[2,1024,3,8,64]{1,4,3,0,2:T(8,128)} fusion(f32[2,1024,3,8,64]{1,4,3,2,0:T(8,128)} %get-tuple-element.64), kind=kLoop, calls=%fused_computation.22 | loop fusion | flops 3145728 | bytes 25165824 | tf_op jit(solution)/shard_map/jit(clip)/min | solution.py:436
  125.2 4.3 slice_bitcast_fusion.1
  129.5 2.5 subtract_convert_fusion.1
  132.0 32.5 %fusion.151 = (f32[2,8,1024]{2,1,0:T(8,128)S(1)}, f32[2,8,1024,1024]{2,3,1,0:T(8,128)}) fusion(pred[1024,1024]{0,1:T(8,128)(4,1)} %iota_compare_fusion, bf16[2,1024,8,32]{1,3,2,0:T(8,128)(2,1)S(1)} %get-tuple-element.56, bf16[2,1024,8,32]{1,3,2,0:T(8,128)(2,1)} %get-tuple-element.57, bf16[2,1024,8,32]{1,3,2,0:T(8,128)(2,1)S(1)} %get-tuple-element.51, ...), kind=kOutput, calls=%fused_computation.166 | convolution fusion | flops 2222982144 | bytes 72417280 | tf_op jit(solution)/shard_map/sub | solution.py:441
  164.6 23.8 %fusion.110 = bf16[2,8,64,1024]{3,2,1,0:T(8,128)(2,1)S(1)} fusion(f32[2,1024,3,8,64]{1,4,3,0,2:T(8,128)} %copy_clamp_fusion, f32[2,8,1024,1024]{2,3,1,0:T(8,128)} %get-tuple-element.62, f32[2,8,1024]{2,1,0:T(8,128)S(1)} %get-tuple-element.61), kind=kOutput, calls=%fused_computation.130 | convolution fusion | flops 2182086656 | bytes 71368704 | tf_op jit(solution)/shard_map/bhqk,bkhe->bqhe/dot_general | solution.py:443
  188.4 5.7 convolution_bitcast_fusion
  194.2 12.1 %reshape_reshape.20 = bf16[1024,2,1408]{2,1,0:T(2,128)(2,1)} reshape(bf16[4,4,4,16,2816]{4,3,2,1,0:T(8,128)(2,1)} %get-tuple-element.16) | data formatting | bytes 11534336 | tf_op jit(solution)/shard_map/reshape;reshape | solution.py:429
  206.3 32.7 %all-reduce.5.cloned.1.call-done = f32[2,1024,1024]{2,1,0:T(8,128)} async-done(((f32[2,1024,1024]{2,1,0:T(8,128)}), f32[2,1024,1024]{2,1,0:T(8,128)}) %all-reduce.5.cloned.1.call-update) | async-done | bytes 8388624 | tf_op jit(solution)/shard_map/psum | solution.py:445
  239.0 5.8 convert_reduce_fusion
  246.2 15.7 %fusion.71 = f32[2,1024,2,1408]{3,1,2,0:T(8,128)} fusion(bf16[1024,2,1408]{2,1,0:T(2,128)(2,1)S(1)} %copy-done.6, bf16[2,1024,1024]{2,1,0:T(8,128)(2,1)S(1)} %get-tuple-element.41, f32[2,1024]{1,0:T(2,128)S(1)} %add_rsqrt_fusion, f32[2,1024]{1,0:T(2,128)S(1)} %broadcast_multiply_fusion.4), kind=kOutput, calls=%fused_computation.88 | convolution fusion | flops 11819548672 | bytes 33046528 | tf_op jit(solution)/shard_map/btd,dcf->btcf/dot_general | solution.py:449
  261.9 19.1 %fusion.65 = (bf16[2,1024,1,1408]{3,1,0,2:T(8,128)(2,1)}, bf16[2,1024,1,1408]{3,1,0,2:T(8,128)(2,1)}) fusion(f32[2,1024,2,1408]{3,1,2,0:T(8,128)} %fusion.71, bf16[1024,1408,1]{1,0,2:T(8,128)(2,1)} %bitcast.236, bf16[2,1024,1024]{2,1,0:T(8,128)(2,1)} %param.7), kind=kOutput, calls=%fused_computation.83 | convolution fusion | flops 5943066624 | bytes 41680896 | tf_op jit(solution)/shard_map/btd,df->btf/dot_general | solution.py:460
  281.0 18.2 %fusion.86 = f32[2,1024,1024]{2,1,0:T(8,128)} fusion(bf16[1024,2,1408,1]{2,1,0,3:T(2,128)(2,1)} %bitcast.228, bf16[2,1024,1,1408]{3,1,0,2:T(8,128)(2,1)} %get-tuple-element.43, bf16[2,1024,1,1408]{3,1,0,2:T(8,128)(2,1)} %get-tuple-element.42), kind=kOutput, calls=%fused_computation.106 | convolution fusion | flops 11816927232 | bytes 25690112 | tf_op jit(solution)/shard_map/btcf,dcf->btd/dot_general | solution.py:465
  299.3 14.1 %fusion.69 = f32[2,1024,1024]{2,1,0:T(8,128)} fusion(bf16[1024,1408,1]{1,0,2:T(8,128)(2,1)} %bitcast.237, f32[2,1024,2,1408]{3,1,2,0:T(8,128)} %fusion.71), kind=kOutput, calls=%fused_computation.86 | convolution fusion | flops 5922881536 | bytes 34340864 | tf_op jit(solution)/shard_map/btf,df->btd/dot_general | solution.py:455
  313.4 29.3 %all-reduce.7.cloned.1.call-done = f32[2,1024,1024]{2,1,0:T(8,128)} async-done(((f32[2,1024,1024]{2,1,0:T(8,128)}), f32[2,1024,1024]{2,1,0:T(8,128)}) %all-reduce.7.cloned.1.call-update) | async-done | bytes 8388624 | tf_op jit(solution)/shard_map/psum | solution.py:465
  342.7 5.9 fusion.149
  348.7 2.4 copy-done.5
  351.0 4.9 fusion.47
  355.9 3.3 copy-done.3
  359.2 2.4 fusion.113
  361.6 24.6 %fusion.96 = bf16[2,1024,1,8,64]{1,4,3,2,0:T(8,128)(2,1)} fusion(bf16[2,1024,8,64]{1,3,2,0:T(8,128)(2,1)S(1)} %fusion.113, f32[2,8,1024,1024]{2,3,1,0:T(8,128)} %get-tuple-element.62, f32[2,8,1024]{2,1,0:T(8,128)S(1)} %get-tuple-element.61), kind=kOutput, calls=%fused_computation.112 | convolution fusion | flops 2181038080 | bytes 71368704 | tf_op jit(solution)/shard_map/bhqk,bqhe->bkhe/dot_general | solution.py:471
  386.2 25.5 %fusion.123 = f32[2,8,1024,1024]{2,3,1,0:T(8,128)} fusion(bf16[2,1024,8,64]{1,3,2,0:T(8,128)(2,1)S(1)} %fusion.113, f32[2,1024,3,8,64]{1,4,3,0,2:T(8,128)} %copy_clamp_fusion), kind=kOutput, calls=%fused_computation.135 | convolution fusion | flops 2147483648 | bytes 71303168 | tf_op jit(solution)/shard_map/bqhe,bkhe->bhqk/dot_general | solution.py:470
  411.7 83.4 %fusion.99 = f32[2,1024,8,64]{1,3,2,0:T(8,128)} fusion(f32[2,8,1024,1024]{2,3,1,0:T(8,128)} %fusion.123, bf16[2,1024,8,32]{1,3,2,0:T(8,128)(2,1)S(1)} %copy-done.17, bf16[2,1024,8,32]{1,3,2,0:T(8,128)(2,1)} %get-tuple-element.57, f32[2,8,1024,1024]{2,3,1,0:T(8,128)} %get-tuple-element.62, f32[2,8,1024]{2,1,0:T(8,128)S(1)} %get-tuple-element.61), kind=kOutput, calls=%fused_computation.113 | convolution fusion | flops 2269135872 | bytes 140574720 | tf_op jit(solution)/shard_map/bhqk,bkhe->bqhe/dot_general | solution.py:474
  495.2 82.9 %fusion.102 = f32[2,1024,8,64]{1,3,2,0:T(8,128)} fusion(f32[2,8,1024,1024]{2,3,1,0:T(8,128)} %fusion.123, bf16[2,1024,8,32]{1,3,2,0:T(8,128)(2,1)S(1)} %copy-done.15, bf16[2,1024,8,32]{1,3,2,0:T(8,128)(2,1)S(1)} %copy-done.13, f32[2,8,1024,1024]{2,3,1,0:T(8,128)} %get-tuple-element.62, f32[2,8,1024]{2,1,0:T(8,128)S(1)} %get-tuple-element.61), kind=kOutput, calls=%fused_computation.114 | convolution fusion | flops 2269135872 | bytes 140574720 | tf_op jit(solution)/shard_map/bhqk,bqhe->bkhe/dot_general | solution.py:475
  578.1 5.0 multiply_subtract_fusion.1
  585.3 16.0 %fusion.83 = f32[2,1024,1024]{2,1,0:T(8,128)} fusion(bf16[1024,3,8,64,1]{3,2,1,0,4:T(8,128)(2,1)S(1)} %bitcast.227, bf16[2,1024,1,8,64]{1,4,3,2,0:T(8,128)(2,1)S(1)} %copy-done.33, bf16[2,1024,1,8,64]{1,4,3,2,0:T(8,128)(2,1)S(1)} %maximum_bitcast_fusion.1, bf16[2,1024,1,8,64]{1,4,3,2,0:T(8,128)(2,1)S(1)} %maximum_bitcast_fusion, ...), kind=kOutput, calls=%fused_computation.105 | convolution fusion | flops 6477053952 | bytes 18219008 | tf_op jit(solution)/shard_map/btchn,dchn->btd/dot_general | solution.py:479
  602.0 18.9 %fusion.61 = f32[1024,2,1408]{2,0,1:T(8,128)S(1)} fusion(bf16[2,1024,1,1408]{3,1,0,2:T(8,128)(2,1)} %get-tuple-element.43, bf16[2,1024,1,1408]{3,1,0,2:T(8,128)(2,1)} %get-tuple-element.42, bf16[2,1024,1024]{2,1,0:T(8,128)(2,1)} %copy-done.1, f32[2,1024]{1,0:T(2,128)S(1)} %copy-done.29, f32[2,1024]{1,0:T(2,128)S(1)} %copy-done.22), kind=kOutput, calls=%fused_computation.79 | convolution fusion | flops 11842617344 | bytes 27279360 | tf_op jit(solution)/shard_map/btd,btcf->dcf/dot_general | solution.py:464
  620.9 10.2 %copy.63 = f32[1024,2,1408]{2,1,0:T(2,128)} copy(f32[1024,2,1408]{2,0,1:T(8,128)S(1)} %fusion.61) | data formatting | bytes 23068672 | tf_op jit(solution)/shard_map/btd,btcf->dcf/dot_general | solution.py:464
  631.1 15.3 %reshape_reshape.23.refs_2_ = f32[4,4,4,16,2816]{4,3,2,1,0:T(8,128)} reshape(f32[1024,2,1408]{2,1,0:T(2,128)} %copy.63) | data formatting | bytes 23068672 | tf_op jit(solution)/shard_map/reshape;reshape | solution.py:384
  646.4 15.1 %fusion.66 = f32[1408,1024,1]{0,1,2:T(8,128)} fusion(bf16[2,1024,1024]{2,1,0:T(8,128)(2,1)} %param.7, f32[2,1024,2,1408]{3,1,2,0:T(8,128)} %fusion.71), kind=kOutput, calls=%fused_computation.84 | convolution fusion | flops 5922881536 | bytes 33030144 | tf_op jit(solution)/shard_map/btd,btf->df/dot_general | solution.py:459
  661.5 5.7 fusion.116
  667.3 2.8 copy.61
  670.1 5.0 reshape_reshape.22.refs_1_
  675.1 14.0 %convolution_bitcast_fusion.1 = f32[1024,3,8,64]{0,3,2,1:T(8,128)} fusion(bf16[2,1024,1024]{2,1,0:T(8,128)(2,1)} %param.6, f32[2,1024]{1,0:T(2,128)S(1)} %copy-done.27, f32[2,1024]{1,0:T(2,128)S(1)} %copy-done.20, bf16[2,1024,1,8,64]{1,4,3,2,0:T(8,128)(2,1)} %fusion.96, bf16[2,1024,1,8,64]{1,4,3,2,0:T(8,128)(2,1)} %copy-done.8, ...), kind=kOutput, calls=%fused_computation.111 | convolution fusion | flops 6485442560 | bytes 17186816 | tf_op jit(solution)/shard_map/btd,btchn->dchn/dot_general | solution.py:478
  689.2 9.8 %copy.59 = f32[1024,3,8,64]{3,2,1,0:T(8,128)} copy(f32[1024,3,8,64]{0,3,2,1:T(8,128)} %convolution_bitcast_fusion.1) | data formatting | bytes 12582912 | tf_op jit(solution)/shard_map/btd,btchn->dchn/dot_general | solution.py:478
  699.0 11.1 %reshape_reshape.21.refs_0_ = f32[4,4,4,16,1536]{4,3,2,1,0:T(8,128)} reshape(f32[1024,3,8,64]{3,2,1,0:T(8,128)} %copy.59) | data formatting | bytes 12582912 | tf_op jit(solution)/shard_map/reshape;reshape | solution.py:384
  710.1 108.4 %torus_scatter.1 = (f32[16,1536]{1,0:T(8,128)}, f32[16,512]{1,0:T(8,128)}, f32[16,2816]{1,0:T(8,128)}, f32[16,1408]{1,0:T(8,128)}) custom-call(f32[4,4,4,16,1536]{4,3,2,1,0:T(8,128)} %reshape_reshape.21.refs_0_, f32[4,4,4,16,512]{4,3,2,1,0:T(8,128)} %reshape_reshape.22.refs_1_, f32[4,4,4,16,2816]{4,3,2,1,0:T(8,128)} %reshape_reshape.23.refs_2_, ...), custom_call_target="tpu_custom_call" | custom-call | tf_op jit(solution)/shard_map/torus_scatter/pallas_call | solution.py:376
  821.6 1.7 reshape.156
  823.3 8.5 %fusion.56 = bf16[2,1024,1024]{2,1,0:T(8,128)(2,1)} fusion(f32[2,1024,1024]{2,1,0:T(8,128)} %get-tuple-element.38, bf16[2,1024,1024]{2,1,0:T(8,128)(2,1)} %copy-done.1), kind=kLoop, calls=%fused_computation.75 | loop fusion | flops 6291456 | bytes 16777216 | tf_op jit(solution)/shard_map/convert_element_type | solution.py:456
  833.1 2.3 fusion.148
  835.4 6.1 fusion.53
  (103 shorter events, 14.3 us)
Async XLA Ops:
  7.2 7.2 copy-start.30
  7.2 7.9 copy-start.23
  7.2 8.7 %copy-start.24 = (bf16[16,2,1408]{2,1,0:T(2,128)(2,1)S(1)}, bf16[16,2,1408]{2,1,0:T(2,128)(2,1)}, u32[]{:S(2)}) copy-start(bf16[16,2,1408]{2,1,0:T(2,128)(2,1)} %param.10) | copy-start | bytes 270340
  7.2 231.8 %all-reduce.5.cloned.1.call-start = ((), (), s32[]{:S(2)}) async-start(), calls=%async_computation | async-start | bytes 16777216 | tf_op jit(solution)/shard_map/psum | solution.py:445
  11.4 88.0 %copy-start.19 = (f32[2,1024]{1,0:T(2,128)}, f32[2,1024]{1,0:T(2,128)S(1)}, u32[]{:S(2)}) copy-start(f32[2,1024]{1,0:T(2,128)S(1)} %broadcast_multiply_fusion.5) | copy-start | bytes 24580
  14.4 85.0 %copy-start.26 = (f32[2,1024]{1,0:T(2,128)}, f32[2,1024]{1,0:T(2,128)S(1)}, u32[]{:S(2)}) copy-start(f32[2,1024]{1,0:T(2,128)S(1)} %add_rsqrt_fusion.1) | copy-start | bytes 24580
  17.7 111.7 %copy-start.9 = (f32[1024,32]{0,1:T(8,128)}, f32[1024,32]{0,1:T(8,128)S(1)}, u32[]{:S(2)}) copy-start(f32[1024,32]{0,1:T(8,128)S(1)} %get-tuple-element.60) | copy-start | bytes 393220
  132.0 32.5 %copy-start.12 = (bf16[2,1024,8,32]{1,3,2,0:T(8,128)(2,1)}, bf16[2,1024,8,32]{1,3,2,0:T(8,128)(2,1)S(1)}, u32[]{:S(2)}) copy-start(bf16[2,1024,8,32]{1,3,2,0:T(8,128)(2,1)S(1)} %get-tuple-element.50) | copy-start | bytes 3145732
  132.0 32.5 %copy-start.14 = (bf16[2,1024,8,32]{1,3,2,0:T(8,128)(2,1)}, bf16[2,1024,8,32]{1,3,2,0:T(8,128)(2,1)S(1)}, u32[]{:S(2)}) copy-start(bf16[2,1024,8,32]{1,3,2,0:T(8,128)(2,1)S(1)} %get-tuple-element.51) | copy-start | bytes 3145732
  132.0 32.5 %copy-start.16 = (bf16[2,1024,8,32]{1,3,2,0:T(8,128)(2,1)}, bf16[2,1024,8,32]{1,3,2,0:T(8,128)(2,1)S(1)}, u32[]{:S(2)}) copy-start(bf16[2,1024,8,32]{1,3,2,0:T(8,128)(2,1)S(1)} %get-tuple-element.56) | copy-start | bytes 3145732
  164.6 23.8 %copy-start.11 = (bf16[1024,8,64]{0,2,1:T(8,128)(2,1)S(1)}, bf16[1024,8,64]{0,2,1:T(8,128)(2,1)}, u32[]{:S(2)}) copy-start(bf16[1024,8,64]{0,2,1:T(8,128)(2,1)} %copy.43) | copy-start | bytes 3145732
  188.4 5.7 copy-start.31
  194.2 148.5 %all-reduce.7.cloned.1.call-start = ((), (), s32[]{:S(2)}) async-start(), calls=%async_computation.1 | async-start | bytes 16777216 | tf_op jit(solution)/shard_map/psum | solution.py:465
  239.0 7.2 copy-start.6
  244.7 17.2 %copy-start.1 = (bf16[2,1024,1024]{2,1,0:T(8,128)(2,1)}, bf16[2,1024,1024]{2,1,0:T(8,128)(2,1)S(1)}, u32[]{:S(2)}) copy-start(bf16[2,1024,1024]{2,1,0:T(8,128)(2,1)S(1)} %get-tuple-element.41) | copy-start | bytes 12582916
  244.7 103.9 %copy-start.21 = (f32[2,1024]{1,0:T(2,128)}, f32[2,1024]{1,0:T(2,128)S(1)}, u32[]{:S(2)}) copy-start(f32[2,1024]{1,0:T(2,128)S(1)} %broadcast_multiply_fusion.4) | copy-start | bytes 24580
  246.2 102.5 %copy-start.28 = (f32[2,1024]{1,0:T(2,128)}, f32[2,1024]{1,0:T(2,128)S(1)}, u32[]{:S(2)}) copy-start(f32[2,1024]{1,0:T(2,128)S(1)} %add_rsqrt_fusion) | copy-start | bytes 24580
  299.2 524.1 %all-reduce.9.cloned.1.call-start = ((), (), s32[]{:S(2)}) async-start(), calls=%async_computation.2 | async-start | bytes 33554432 | tf_op jit(solution)/shard_map/psum | solution.py:456
  342.7 6.0 copy-start.2
  342.7 8.3 copy-start.5
  355.9 3.3 copy-start.3
  386.2 25.5 %copy-start.17 = (bf16[2,1024,8,32]{1,3,2,0:T(8,128)(2,1)S(1)}, bf16[2,1024,8,32]{1,3,2,0:T(8,128)(2,1)}, u32[]{:S(2)}) copy-start(bf16[2,1024,8,32]{1,3,2,0:T(8,128)(2,1)} %copy-done.16) | copy-start | bytes 3145732
  411.7 83.4 %copy-start.13 = (bf16[2,1024,8,32]{1,3,2,0:T(8,128)(2,1)S(1)}, bf16[2,1024,8,32]{1,3,2,0:T(8,128)(2,1)}, u32[]{:S(2)}) copy-start(bf16[2,1024,8,32]{1,3,2,0:T(8,128)(2,1)} %copy-done.12) | copy-start | bytes 3145732
  411.7 83.4 %copy-start.15 = (bf16[2,1024,8,32]{1,3,2,0:T(8,128)(2,1)S(1)}, bf16[2,1024,8,32]{1,3,2,0:T(8,128)(2,1)}, u32[]{:S(2)}) copy-start(bf16[2,1024,8,32]{1,3,2,0:T(8,128)(2,1)} %copy-done.14) | copy-start | bytes 3145732
  495.1 82.9 %copy-start.10 = (f32[1024,32]{0,1:T(8,128)S(1)}, f32[1024,32]{0,1:T(8,128)}, u32[]{:S(2)}) copy-start(f32[1024,32]{0,1:T(8,128)} %copy-done.9) | copy-start | bytes 393220
  495.1 82.9 %copy-start.18 = (f32[1024,32]{0,1:T(8,128)S(1)}, f32[1024,32]{0,1:T(8,128)}, u32[]{:S(2)}) copy-start(f32[1024,32]{0,1:T(8,128)} %get-tuple-element.58) | copy-start | bytes 393220
  578.0 7.3 slice-start
  578.0 7.3 slice-start.1
  578.0 7.3 copy-start.33
  578.1 7.3 copy-start.34
  583.3 1.3 copy-start.7
  583.6 1.8 copy-start.8
  601.3 0.7 copy-start.22
  601.3 0.7 copy-start.29
  646.4 15.1 %copy-start.32 = (bf16[2,8,64,1024]{3,2,1,0:T(8,128)(2,1)S(1)}, bf16[2,8,64,1024]{3,2,1,0:T(8,128)(2,1)}, u32[]{:S(2)}) copy-start(bf16[2,8,64,1024]{3,2,1,0:T(8,128)(2,1)} %copy-done.31) | copy-start | bytes 6291460
  667.2 7.9 copy-start.20
  667.2 7.9 copy-start.27
  667.2 7.9 copy-start.35
  823.3 8.5 %copy-start = (bf16[2,1024,1024]{2,1,0:T(8,128)(2,1)S(1)}, bf16[2,1024,1024]{2,1,0:T(8,128)(2,1)}, u32[]{:S(2)}) copy-start(bf16[2,1024,1024]{2,1,0:T(8,128)(2,1)} %param.6) | copy-start | bytes 12582916
  823.3 9.8 %copy-start.4 = (f32[2,1024,1024]{2,1,0:T(8,128)S(1)}, f32[2,1024,1024]{2,1,0:T(8,128)}, u32[]{:S(2)}) copy-start(f32[2,1024,1024]{2,1,0:T(8,128)} %get-tuple-element.39) | copy-start | bytes 25165828
  835.4 6.1 copy-start.25
Sparse Core Ops, SparseCore 0:
  194.3 44.6 all-reduce.4
  299.4 43.3 all-reduce.6
  601.5 61.4 all-reduce.8
